TPU v7x, 32 devices: a whole 2x2x4 slice. The times are simulated.
32 devices in a mesh: rows: 8 (over z, y), cols: 4 (over x, core).
Axes of the slice: x: 2, y: 2, z: 4, core: 2. Of those that a mesh axis runs over, the one named last changes fastest.
Arguments:
- weight_up: bfloat16 [12288, 49152], P('rows', 'cols'), may hold values from -0.078125 to 0.078125
- low_up: bfloat16 [12288, 64], P('rows'), may hold values from -0.0546875 to 0.0546875
- high_up: bfloat16 [64, 49152], P(None, 'cols'), may hold values from -0.75 to 0.75
- norm_train: float32 [12288], P(('rows', 'cols')), may hold values from 0.25 to 1.75
- norm_step: float32 [12288], P(('rows', 'cols')), may hold values from -0.3 to 0.3
Outputs:
- serve_up: bfloat16 [12288, 49152], P(None, ('cols', 'rows'))
- scale_up: float32 [49152], P(('cols', 'rows'))
- serve_norm: bfloat16 [12288], replicated
All inputs are finite; a program needn't handle non-finite values.
Results may differ from a plain program's by a relative error of at most 0.0004.
Values may be sent and summed in bfloat16 or wider, within the bound.
A program may use at most 256 MiB of HBM per device.

v0:
```python
import functools

import jax
import jax.numpy as jnp
from jax import lax
from jax.experimental import pallas as pl
from jax.experimental.pallas import tpu as pltpu
from jax.sharding import PartitionSpec as P

mix_rate = 0.5
MESH = pl.DeviceIdType.MESH
LANES = 128


def partner(me, step):
    bit, other = 1, me
    while bit <= step:
        if step & bit:
            other = other + bit - 2 * bit * lax.rem(other // bit, 2)
        bit *= 2
    return other


def send_orders(ranks):
    far, near = list(range(ranks - 1, ranks // 2 - 1, -1)), list(range(ranks // 2 - 1, 0, -1))
    half = len(far) // 2
    turned = near[:-1][::-1] + near[-1:]
    return far + near, far[half:] + far[:half] + turned


def exchange(
    ranks, teams, w_ref, low_ref, high_ref, train_ref, step_ref,
    held, scale_out, norm_out,
    scale_ref, norm_ref, small_sem, fresh, norm_all, norms, low_all, high_own,
    send_sem, recv_sem, own_sem, high_sem,
    low_send, low_recv, low_own, norm_send, norm_recv, norm_own,
    low_send2, low_recv2, norm_send2, norm_recv2,
):
    me, team = lax.axis_index("rows"), lax.axis_index("cols")
    rows, columns = w_ref.shape
    share = columns // ranks
    pieces = share // LANES
    part = rows // teams
    half = ranks // 2
    parity = lax.rem(team, 2)
    gains = (train_ref, step_ref)

    def pick(first, second):
        first, second = partner(me, first), partner(me, second)
        return first + parity * (second - first)

    peers = [pick(first, second) for first, second in zip(*send_orders(ranks))]
    arrivals = peers[half:][::-1] + peers[:half]

    def window(owner, piece):
        return pl.ds(pl.multiple_of(owner * share + piece * LANES, LANES), LANES)

    def block(owner):
        return pl.ds(pl.multiple_of(owner * rows, 16), rows)

    def piece_copy(piece, to, source_rank):
        return pltpu.make_async_remote_copy(
            src_ref=w_ref.at[:, window(to, piece)],
            dst_ref=held.at[piece, block(me)],
            send_sem=send_sem.at[piece, to],
            recv_sem=recv_sem.at[piece, source_rank],
            device_id={"rows": to},
            device_id_type=MESH,
        )

    def piece_own(piece):
        return pltpu.make_async_copy(
            w_ref.at[:, window(me, piece)], held.at[piece, block(me)], own_sem.at[piece]
        )

    def issue(piece):
        for to in peers:
            piece_copy(piece, to, me).start()
        piece_own(piece).start()

    low_mine = low_ref.at[:, pl.ds(pl.multiple_of(team * part, LANES), part)]

    def low_copy(source, owner, to, sem):
        return pltpu.make_async_remote_copy(
            src_ref=source,
            dst_ref=low_all.at[team, owner],
            send_sem=low_send.at[sem],
            recv_sem=low_recv.at[owner],
            device_id={"rows": to},
            device_id_type=MESH,
        )

    def norm_copy(which, to, source_rank):
        return pltpu.make_async_remote_copy(
            src_ref=gains[which],
            dst_ref=norm_all.at[which, team, me],
            send_sem=norm_send.at[which, to],
            recv_sem=norm_recv.at[which, source_rank],
            device_id={"rows": to},
            device_id_type=MESH,
        )

    def team_copy(buffer, sends, receives, to, source_team):
        return pltpu.make_async_remote_copy(
            src_ref=buffer.at[team],
            dst_ref=buffer.at[team],
            send_sem=sends.at[to],
            recv_sem=receives.at[source_team],
            device_id={"cols": to},
            device_id_type=MESH,
        )

    high_copy = pltpu.make_async_copy(
        high_ref.at[:, pl.ds(pl.multiple_of(me * share, LANES), share)], high_own, high_sem
    )
    high_copy.start()
    low_keep = pltpu.make_async_copy(low_mine, low_all.at[team, me], low_own)
    low_keep.start()
    norm_keep = [
        pltpu.make_async_copy(gains[which], norm_all.at[which, team, me], norm_own.at[which])
        for which in range(2)
    ]
    for copy in norm_keep:
        copy.start()

    barrier = pltpu.get_barrier_semaphore()
    for step in range(1, ranks):
        pl.semaphore_signal(
            barrier, inc=1, device_id={"rows": partner(me, step)}, device_id_type=MESH
        )
    for step in range(1, teams):
        pl.semaphore_signal(
            barrier, inc=1, device_id={"cols": lax.rem(team + step, teams)}, device_id_type=MESH
        )
    pl.semaphore_wait(barrier, ranks - 1 + teams - 1)

    across = partner(me, half)
    direct = [half] + list(range(1, half))
    for step in direct:
        low_copy(low_mine, me, partner(me, step), step).start()
    for step in range(1, ranks):
        for which in range(2):
            norm_copy(which, partner(me, step), me).start()

    issue(0)

    low_copy(low_mine, across, across, half).wait_recv()
    for step in range(1, half):
        low_copy(low_all.at[team, across], across, partner(me, step), half + step).start()

    @pl.loop(1, pieces)
    def _(piece):
        issue(piece)

    low_keep.wait()
    for copy in norm_keep:
        copy.wait()
    for step in direct:
        low_copy(low_mine, me, partner(me, step), step).wait_send()
    for step in range(1, half):
        low_copy(low_mine, partner(me, step), across, step).wait_recv()
        low_copy(low_mine, partner(me, half + step), across, step).wait_recv()
        low_copy(low_all.at[team, across], across, partner(me, step), half + step).wait_send()
    for step in range(1, ranks):
        for which in range(2):
            norm_copy(which, partner(me, step), partner(me, step)).wait()
    high_copy.wait()

    gathers = [(low_all, low_send2, low_recv2)] + [
        (norm_all.at[which], norm_send2.at[which], norm_recv2.at[which]) for which in range(2)
    ]
    for step in range(1, teams):
        for gather in gathers:
            team_copy(*gather, lax.rem(team + step, teams), team).start()
    for step in range(1, teams):
        to, back = lax.rem(team + step, teams), lax.rem(team + teams - step, teams)
        for gather in gathers:
            team_copy(*gather, to, back).wait()

    height = train_ref.shape[0]
    for rank in range(ranks):
        for mate in range(teams):
            at = (rank * teams + mate) * height
            norms[at:at + height, :] = norm_all[0, mate, rank] + norm_all[1, mate, rank]
    norm_ref[...] = norms[...].astype(jnp.bfloat16)
    norm_put = pltpu.make_async_copy(norm_ref, norm_out, small_sem.at[1])
    norm_put.start()

    def gather_block(piece, owner, total):
        high = high_own[:, pl.ds(pl.multiple_of(piece * LANES, LANES), LANES)]

        def one(quarter, total):
            added = lax.dot_general(
                low_all[quarter, owner], high, (((0,), (0,)), ((), ())),
                preferred_element_type=jnp.float32,
            )
            span = pl.ds(pl.multiple_of(owner * rows + quarter * part, 16), part)
            now = held[piece, span, :].astype(jnp.float32) + mix_rate * added
            fresh[span, :] = now
            return total + jnp.sum((now * now).reshape(part // 8, 8, LANES), axis=0)

        return lax.fori_loop(0, teams, one, total)

    def gather(piece):
        piece_own(piece).wait()
        total = gather_block(piece, me, jnp.zeros((8, LANES), jnp.float32))
        for back in arrivals:
            piece_copy(piece, back, back).wait_recv()
            total = gather_block(piece, back, total)
        scale = jnp.sqrt(jnp.sum(total, axis=0, keepdims=True))
        scale_ref[pl.ds(piece, 1), :] = scale
        return scale

    @pl.loop(0, pieces)
    def _(piece):
        inverse = 1.0 / gather(piece)

        @pl.loop(0, ranks * teams)
        def _(index):
            span = pl.ds(pl.multiple_of(index * part, 16), part)
            held[piece, span, :] = (fresh[span, :] * inverse).astype(jnp.bfloat16)

    scale_put = pltpu.make_async_copy(scale_ref, scale_out, small_sem.at[0])
    scale_put.start()

    @pl.loop(0, pieces)
    def _(piece):
        for to in peers:
            piece_copy(piece, to, me).wait_send()
    norm_put.wait()
    scale_put.wait()


def write_out(held, serve_ref, out_sem):
    copies = [
        pltpu.make_async_copy(
            held.at[piece], serve_ref.at[:, pl.ds(piece * LANES, LANES)], out_sem.at[piece]
        )
        for piece in range(held.shape[0])
    ]
    for copy in copies:
        copy.start()
    for copy in copies:
        copy.wait()


def with_kernel(ranks, teams, weight_up, low_up, high_up, norm_train, norm_step):
    rows, columns = weight_up.shape
    rank = low_up.shape[1]
    share = columns // ranks
    pieces = share // LANES
    part = rows // teams
    height = norm_train.shape[0] // LANES
    dma = pltpu.SemaphoreType.DMA
    anywhere, vmem = pl.BlockSpec(memory_space=pl.ANY), pl.BlockSpec(memory_space=pltpu.VMEM)
    shapes = (
        ((ranks * rows, share), jnp.bfloat16),
        ((pieces, LANES), jnp.float32),
        ((ranks * teams * height, LANES), jnp.bfloat16),
    )
    held, scale_up, serve_norm = pl.pallas_call(
        functools.partial(exchange, ranks, teams),
        out_shape=(
            pltpu.VMEM((pieces, ranks * rows, LANES), jnp.bfloat16),
            *[jax.ShapeDtypeStruct(*shape) for shape in shapes[1:]],
        ),
        in_specs=[anywhere] * 5,
        out_specs=(vmem, anywhere, anywhere),
        scratch_shapes=[
            *[pltpu.VMEM(*shape) for shape in shapes[1:]],
            dma((2,)),
            pltpu.VMEM((ranks * rows, LANES), jnp.float32),
            pltpu.VMEM((2, teams, ranks, height, LANES), jnp.float32),
            pltpu.VMEM((ranks * teams * height, LANES), jnp.float32),
            pltpu.VMEM((teams, ranks, rank, part), jnp.bfloat16),
            pltpu.VMEM((rank, share), jnp.bfloat16),
            dma((pieces, ranks)), dma((pieces, ranks)), dma((pieces,)), dma,
            dma((2 * ranks,)), dma((ranks,)), dma, dma((2, ranks)), dma((2, ranks)), dma((2,)),
            dma((teams,)), dma((teams,)), dma((2, teams)), dma((2, teams)),
        ],
        compiler_params=pltpu.CompilerParams(
            collective_id=0, has_side_effects=True, vmem_limit_bytes=20 * 1024 * 1024
        ),
    )(
        weight_up, low_up.T, high_up,
        norm_train.reshape(height, LANES), norm_step.reshape(height, LANES),
    )
    serve_up = pl.pallas_call(
        write_out,
        out_shape=jax.ShapeDtypeStruct(*shapes[0]),
        in_specs=[anywhere],
        out_specs=anywhere,
        scratch_shapes=[dma((pieces,))],
        compiler_params=pltpu.CompilerParams(vmem_limit_bytes=1024 * 1024),
    )(held)
    return serve_up, scale_up.reshape(-1), serve_norm.reshape(-1)


def with_collectives(weight_up, low_up, high_up, norm_train, norm_step):
    fresh_up = weight_up.astype(jnp.float32) + mix_rate * jnp.dot(
        low_up, high_up, preferred_element_type=jnp.float32
    )
    total_up = lax.psum(jnp.sum(fresh_up * fresh_up, axis=0), "rows")
    scale_up = jnp.sqrt(total_up)
    narrow_up = (fresh_up / scale_up).astype(jnp.bfloat16)
    serve_up = lax.all_to_all(narrow_up, "rows", split_axis=1, concat_axis=0, tiled=True)
    place = lax.axis_index("rows")
    scale_up = lax.dynamic_slice_in_dim(scale_up, place * serve_up.shape[1], serve_up.shape[1])
    serve_norm = lax.all_gather(
        (norm_train + norm_step).astype(jnp.bfloat16), ("rows", "cols"), axis=0, tiled=True
    )
    return (serve_up, scale_up, serve_norm)


def solution(mesh):
    ranks, teams = mesh.shape["rows"], mesh.shape["cols"]

    def per_device(weight_up, low_up, high_up, norm_train, norm_step):
        rows, columns = weight_up.shape
        share = columns // ranks
        aligned = (
            share % LANES == 0 and rows % (LANES * teams) == 0
            and ranks & (ranks - 1) == 0 and norm_train.shape[0] % LANES == 0
        )
        fits = 2 * ranks * rows * share < 40 * 1024 * 1024
        if aligned and fits:
            return with_kernel(ranks, teams, weight_up, low_up, high_up, norm_train, norm_step)
        return with_collectives(weight_up, low_up, high_up, norm_train, norm_step)

    in_specs = (
        P("rows", "cols"),
        P("rows", None),
        P(None, "cols"),
        P(("rows", "cols")),
        P(("rows", "cols")),
    )
    out_specs = (P(None, ("cols", "rows")), P(("cols", "rows")), P())
    return jax.shard_map(
        per_device, mesh=mesh, in_specs=in_specs, out_specs=out_specs, check_vma=False
    )
```

profile of v0, /device:TPU:0, one launch (start us, length us, event | category | flops | bytes accessed | tf_op | source)
XLA Modules:
  0.0 837.8 jit_solution(17554780163060306855)
XLA Ops:
  0.6 823.5 %shard_map.76 = (bf16[12,12288,128]{2,1,0:T(8,128)(2,1)S(1)}, f32[12,128]{1,0:T(8,128)}, bf16[96,128]{1,0:T(8,128)(2,1)}) custom-call(bf16[1536,12288]{1,0:T(8,128)(2,1)} %w_ref.1, bf16[64,1536]{1,0:T(8,128)(2,1)} %bitcast.5, bf16[64,12288]{1,0:T(8,128)(2,1)} %high_ref.1, f32[3,128]{1,0:T(4,128)} %bitcast.8, f32[3,128]{1,0:T(4,128)} %bitcast.9), custom_call_target="tpu_custom_call" | custom-call | tf_op jit(solution)/shard_map/pallas_call | solution.py:261
  824.2 0.0 copy-start.1
  824.2 0.0 copy-start
  824.2 12.4 %shard_map.77 = bf16[12288,1536]{1,0:T(8,128)(2,1)} custom-call(bf16[12,12288,128]{2,1,0:T(8,128)(2,1)S(1)} %get-tuple-element.6.held), custom_call_target="tpu_custom_call" | custom-call | tf_op jit(solution)/shard_map/pallas_call | solution.py:288
  836.5 0.0 copy-done.1
  836.5 0.6 copy.10
  837.1 0.0 copy-done
  837.1 0.6 copy.11
Async XLA Ops:
  824.2 12.4 %copy-start.1 = (f32[12,128]{1,0:T(8,128)S(1)}, f32[12,128]{1,0:T(8,128)}, u32[]{:S(2)}) copy-start(f32[12,128]{1,0:T(8,128)} %get-tuple-element.7) | copy-start | bytes 18436
  824.2 13.0 %copy-start = (bf16[96,128]{1,0:T(8,128)(2,1)S(1)}, bf16[96,128]{1,0:T(8,128)(2,1)}, u32[]{:S(2)}) copy-start(bf16[96,128]{1,0:T(8,128)(2,1)} %get-tuple-element.8) | copy-start | bytes 73732
where the time goes:
time: 838 us
  Pallas kernels  836 us (100%)
    pallas_call x1, Pallas kernels, with_kernel(): pl.pallas_call(functools.partial(exchange, ranks, teams), out_shape=(pltp...  824 us

commit v1 on v0

v1 whole, which is shorter than its diff:
```python
import functools

import jax
import jax.numpy as jnp
from jax import lax
from jax.experimental import pallas as pl
from jax.experimental.pallas import tpu as pltpu
from jax.sharding import PartitionSpec as P

mix_rate = 0.5
MESH = pl.DeviceIdType.MESH
LANES = 128


def partner(me, step):
    bit, other = 1, me
    while bit <= step:
        if step & bit:
            other = other + bit - 2 * bit * lax.rem(other // bit, 2)
        bit *= 2
    return other


def send_orders(ranks):
    far, near = list(range(ranks - 1, ranks // 2 - 1, -1)), list(range(ranks // 2 - 1, 0, -1))
    half = len(far) // 2
    turned = near[:-1][::-1] + near[-1:]
    return far + near, far[half:] + far[:half] + turned


def cut(pieces):
    return pieces - 2 + lax.rem(lax.axis_index("cols"), 2)


def exchange(ranks, teams, first, *refs):
    if first:
        (
            w_ref, low_ref, high_ref, train_ref, step_ref,
            held, scale_out, low_out, norm_out,
            scale_ref, small_sem, fresh, low_all, high_own, send_sem, recv_sem, own_sem, high_sem,
            norm_ref, norm_all, norms,
            low_send, low_recv, low_own, norm_send, norm_recv, norm_own,
            low_send2, low_recv2, norm_send2, norm_recv2,
        ) = refs
        gains = (train_ref, step_ref)
    else:
        (
            w_ref, low_ref, high_ref, scale_in,
            held, scale_out,
            scale_ref, small_sem, fresh, low_all, high_own, send_sem, recv_sem, own_sem, high_sem,
        ) = refs
    me, team = lax.axis_index("rows"), lax.axis_index("cols")
    rows, columns = w_ref.shape
    share = columns // ranks
    pieces = share // LANES
    part = rows // teams
    half = ranks // 2
    parity = lax.rem(team, 2)
    low, high = (0, cut(pieces)) if first else (cut(pieces), pieces)

    def pick(one, other):
        one, other = partner(me, one), partner(me, other)
        return one + parity * (other - one)

    peers = [pick(one, other) for one, other in zip(*send_orders(ranks))]
    arrivals = peers[half:][::-1] + peers[:half]

    def window(owner, piece):
        return pl.ds(pl.multiple_of(owner * share + piece * LANES, LANES), LANES)

    def block(owner):
        return pl.ds(pl.multiple_of(owner * rows, 16), rows)

    def piece_copy(piece, to, source_rank):
        return pltpu.make_async_remote_copy(
            src_ref=w_ref.at[:, window(to, piece)],
            dst_ref=held.at[piece - low, block(me)],
            send_sem=send_sem.at[piece - low, to],
            recv_sem=recv_sem.at[piece - low, source_rank],
            device_id={"rows": to},
            device_id_type=MESH,
        )

    def piece_own(piece):
        return pltpu.make_async_copy(
            w_ref.at[:, window(me, piece)], held.at[piece - low, block(me)], own_sem.at[piece - low]
        )

    def issue(piece):
        for to in peers:
            piece_copy(piece, to, me).start()
        piece_own(piece).start()

    high_copy = pltpu.make_async_copy(
        high_ref.at[:, pl.ds(pl.multiple_of(me * share, LANES), share)], high_own, high_sem
    )
    high_copy.start()

    def greet(mates):
        barrier = pltpu.get_barrier_semaphore()
        for step in range(1, ranks):
            pl.semaphore_signal(
                barrier, inc=1, device_id={"rows": partner(me, step)}, device_id_type=MESH
            )
        for step in range(1, mates):
            pl.semaphore_signal(
                barrier, inc=1, device_id={"cols": lax.rem(team + step, mates)},
                device_id_type=MESH,
            )
        pl.semaphore_wait(barrier, ranks - 1 + mates - 1)

    def start_first():
        low_mine = low_ref.at[:, pl.ds(pl.multiple_of(team * part, LANES), part)]

        def low_copy(source, owner, to, sem):
            return pltpu.make_async_remote_copy(
                src_ref=source,
                dst_ref=low_all.at[team, owner],
                send_sem=low_send.at[sem],
                recv_sem=low_recv.at[owner],
                device_id={"rows": to},
                device_id_type=MESH,
            )

        def norm_copy(which, to, source_rank):
            return pltpu.make_async_remote_copy(
                src_ref=gains[which],
                dst_ref=norm_all.at[which, team, me],
                send_sem=norm_send.at[which, to],
                recv_sem=norm_recv.at[which, source_rank],
                device_id={"rows": to},
                device_id_type=MESH,
            )

        def team_copy(buffer, sends, receives, to, source_team):
            return pltpu.make_async_remote_copy(
                src_ref=buffer.at[team],
                dst_ref=buffer.at[team],
                send_sem=sends.at[to],
                recv_sem=receives.at[source_team],
                device_id={"cols": to},
                device_id_type=MESH,
            )

        keeps = [pltpu.make_async_copy(low_mine, low_all.at[team, me], low_own)] + [
            pltpu.make_async_copy(gains[which], norm_all.at[which, team, me], norm_own.at[which])
            for which in range(2)
        ]
        for copy in keeps:
            copy.start()
        greet(teams)

        across = partner(me, half)
        direct = [half] + list(range(1, half))
        for step in direct:
            low_copy(low_mine, me, partner(me, step), step).start()
        for step in range(1, ranks):
            for which in range(2):
                norm_copy(which, partner(me, step), me).start()

        issue(low)

        low_copy(low_mine, across, across, half).wait_recv()
        for step in range(1, half):
            low_copy(low_all.at[team, across], across, partner(me, step), half + step).start()

        pl.loop(low + 1, high)(issue)

        for copy in keeps:
            copy.wait()
        for step in direct:
            low_copy(low_mine, me, partner(me, step), step).wait_send()
        for step in range(1, half):
            low_copy(low_mine, partner(me, step), across, step).wait_recv()
            low_copy(low_mine, partner(me, half + step), across, step).wait_recv()
            low_copy(low_all.at[team, across], across, partner(me, step), half + step).wait_send()
        for step in range(1, ranks):
            for which in range(2):
                norm_copy(which, partner(me, step), partner(me, step)).wait()
        high_copy.wait()

        gathers = [(low_all, low_send2, low_recv2)] + [
            (norm_all.at[which], norm_send2.at[which], norm_recv2.at[which]) for which in range(2)
        ]
        for step in range(1, teams):
            for gather in gathers:
                team_copy(*gather, lax.rem(team + step, teams), team).start()
        for step in range(1, teams):
            to, back = lax.rem(team + step, teams), lax.rem(team + teams - step, teams)
            for gather in gathers:
                team_copy(*gather, to, back).wait()

        height = train_ref.shape[0]
        for rank in range(ranks):
            for mate in range(teams):
                at = (rank * teams + mate) * height
                norms[at:at + height, :] = norm_all[0, mate, rank] + norm_all[1, mate, rank]
        norm_ref[...] = norms[...].astype(jnp.bfloat16)
        puts = [
            pltpu.make_async_copy(low_all, low_out, small_sem.at[1]),
            pltpu.make_async_copy(norm_ref, norm_out, small_sem.at[2]),
        ]
        for copy in puts:
            copy.start()
        return puts

    def start_second():
        takes = [
            high_copy,
            pltpu.make_async_copy(low_ref, low_all, small_sem.at[1]),
            pltpu.make_async_copy(scale_in, scale_ref, small_sem.at[2]),
        ]
        for copy in takes[1:]:
            copy.start()
        greet(1)
        pl.loop(low, high)(issue)
        for copy in takes:
            copy.wait()
        return []

    puts = start_first() if first else start_second()

    def gather_block(piece, owner, total):
        now_high = high_own[:, pl.ds(pl.multiple_of(piece * LANES, LANES), LANES)]

        def one(quarter, total):
            added = lax.dot_general(
                low_all[quarter, owner], now_high, (((0,), (0,)), ((), ())),
                preferred_element_type=jnp.float32,
            )
            span = pl.ds(pl.multiple_of(owner * rows + quarter * part, 16), part)
            now = held[piece - low, span, :].astype(jnp.float32) + mix_rate * added
            fresh[span, :] = now
            return total + jnp.sum((now * now).reshape(part // 8, 8, LANES), axis=0)

        return lax.fori_loop(0, teams, one, total)

    @pl.loop(low, high)
    def _(piece):
        piece_own(piece).wait()
        total = gather_block(piece, me, jnp.zeros((8, LANES), jnp.float32))
        for back in arrivals:
            piece_copy(piece, back, back).wait_recv()
            total = gather_block(piece, back, total)
        scale = jnp.sqrt(jnp.sum(total, axis=0, keepdims=True))
        scale_ref[pl.ds(piece, 1), :] = scale
        inverse = 1.0 / scale

        @pl.loop(0, ranks * teams)
        def _(index):
            span = pl.ds(pl.multiple_of(index * part, 16), part)
            held[piece - low, span, :] = (fresh[span, :] * inverse).astype(jnp.bfloat16)

    scale_put = pltpu.make_async_copy(scale_ref, scale_out, small_sem.at[0])
    scale_put.start()

    @pl.loop(low, high)
    def _(piece):
        for to in peers:
            piece_copy(piece, to, me).wait_send()

    scale_put.wait()
    for copy in puts:
        copy.wait()


def window_of(piece):
    return pl.ds(piece * LANES, LANES)


def write_first(held, scale_ref, norm_ref, serve_ref, scale_out, norm_out, out_sem, small_sem):
    pieces = held.shape[0] + 1
    puts = [
        pltpu.make_async_copy(
            held.at[piece], serve_ref.at[:, window_of(piece)], out_sem.at[piece]
        )
        for piece in range(pieces - 1)
    ]
    smalls = [
        pltpu.make_async_copy(scale_ref, scale_out, small_sem.at[0]),
        pltpu.make_async_copy(norm_ref, norm_out, small_sem.at[1]),
    ]
    late = cut(pieces) == pieces - 1
    for copy in smalls + puts[:-1]:
        copy.start()
    pl.when(late)(puts[-1].start)
    for copy in smalls + puts[:-1]:
        copy.wait()
    pl.when(late)(puts[-1].wait)


def write_second(pieces, _, held, scale_ref, serve_ref, scale_out, out_sem, small_sem):
    early = cut(pieces) == pieces - 2
    middle = pltpu.make_async_copy(
        held.at[0], serve_ref.at[:, window_of(pieces - 2)], out_sem.at[0]
    )
    last = pltpu.make_async_copy(
        held.at[pieces - 1 - cut(pieces)], serve_ref.at[:, window_of(pieces - 1)], out_sem.at[1]
    )
    small = pltpu.make_async_copy(scale_ref, scale_out, small_sem)
    small.start()
    last.start()
    pl.when(early)(middle.start)
    small.wait()
    last.wait()
    pl.when(early)(middle.wait)


def with_kernel(ranks, teams, weight_up, low_up, high_up, norm_train, norm_step):
    rows, columns = weight_up.shape
    rank = low_up.shape[1]
    share = columns // ranks
    pieces = share // LANES
    part = rows // teams
    height = norm_train.shape[0] // LANES
    dma = pltpu.SemaphoreType.DMA
    anywhere, vmem = pl.BlockSpec(memory_space=pl.ANY), pl.BlockSpec(memory_space=pltpu.VMEM)
    hbm = pl.BlockSpec(memory_space=pltpu.HBM)

    def keep(*arrays):
        return [pltpu.with_memory_space_constraint(array, pltpu.HBM) for array in arrays]

    serve = jax.ShapeDtypeStruct((ranks * rows, share), jnp.bfloat16)
    scale = pltpu.HBM((pieces, LANES), jnp.float32)
    norm = pltpu.HBM((ranks * teams * height, LANES), jnp.bfloat16)
    lows = pltpu.HBM((teams, ranks, rank, part), jnp.bfloat16)

    def call(first, slots, outs, extra, *operands):
        return pl.pallas_call(
            functools.partial(exchange, ranks, teams, first),
            out_shape=(pltpu.VMEM((slots, ranks * rows, LANES), jnp.bfloat16), *outs),
            in_specs=[hbm] * len(operands),
            out_specs=(vmem, *[hbm] * len(outs)),
            scratch_shapes=[
                pltpu.VMEM(scale.shape, scale.dtype),
                dma((3,)),
                pltpu.VMEM((ranks * rows, LANES), jnp.float32),
                pltpu.VMEM(lows.shape, lows.dtype),
                pltpu.VMEM((rank, share), jnp.bfloat16),
                dma((slots, ranks)), dma((slots, ranks)), dma((slots,)), dma,
                *extra,
            ],
            compiler_params=pltpu.CompilerParams(
                collective_id=0 if first else 1, has_side_effects=True,
                vmem_limit_bytes=20 * 1024 * 1024,
            ),
        )(*keep(*operands))

    held, scale_up, low_all, serve_norm = call(
        True, pieces - 1, (scale, lows, norm),
        [
            pltpu.VMEM(norm.shape, norm.dtype),
            pltpu.VMEM((2, teams, ranks, height, LANES), jnp.float32),
            pltpu.VMEM(norm.shape, jnp.float32),
            dma((ranks,)), dma((ranks,)), dma, dma((2, ranks)), dma((2, ranks)), dma((2,)),
            dma((teams,)), dma((teams,)), dma((2, teams)), dma((2, teams)),
        ],
        weight_up, low_up.T, high_up,
        norm_train.reshape(height, LANES), norm_step.reshape(height, LANES),
    )
    serve_up, scale_up, serve_norm = pl.pallas_call(
        write_first,
        out_shape=(serve, scale, norm),
        in_specs=[anywhere, hbm, hbm],
        out_specs=(anywhere, hbm, hbm),
        scratch_shapes=[dma((pieces - 1,)), dma((2,))],
        compiler_params=pltpu.CompilerParams(vmem_limit_bytes=1024 * 1024),
    )(held, *keep(scale_up, serve_norm))
    held, scale_up = call(False, 2, (scale,), [], weight_up, low_all, high_up, scale_up)
    serve_up, scale_up = pl.pallas_call(
        functools.partial(write_second, pieces),
        out_shape=(serve, scale),
        in_specs=[anywhere, anywhere, hbm],
        out_specs=(anywhere, hbm),
        scratch_shapes=[dma((2,)), dma],
        compiler_params=pltpu.CompilerParams(vmem_limit_bytes=1024 * 1024),
        input_output_aliases={0: 0},
    )(serve_up, held, *keep(scale_up))
    return serve_up, scale_up.reshape(-1), serve_norm.reshape(-1)


def with_collectives(weight_up, low_up, high_up, norm_train, norm_step):
    fresh_up = weight_up.astype(jnp.float32) + mix_rate * jnp.dot(
        low_up, high_up, preferred_element_type=jnp.float32
    )
    total_up = lax.psum(jnp.sum(fresh_up * fresh_up, axis=0), "rows")
    scale_up = jnp.sqrt(total_up)
    narrow_up = (fresh_up / scale_up).astype(jnp.bfloat16)
    serve_up = lax.all_to_all(narrow_up, "rows", split_axis=1, concat_axis=0, tiled=True)
    place = lax.axis_index("rows")
    scale_up = lax.dynamic_slice_in_dim(scale_up, place * serve_up.shape[1], serve_up.shape[1])
    serve_norm = lax.all_gather(
        (norm_train + norm_step).astype(jnp.bfloat16), ("rows", "cols"), axis=0, tiled=True
    )
    return (serve_up, scale_up, serve_norm)


def solution(mesh):
    ranks, teams = mesh.shape["rows"], mesh.shape["cols"]

    def per_device(weight_up, low_up, high_up, norm_train, norm_step):
        rows, columns = weight_up.shape
        share = columns // ranks
        aligned = (
            share % LANES == 0 and share >= 3 * LANES and rows % (LANES * teams) == 0
            and ranks & (ranks - 1) == 0 and norm_train.shape[0] % LANES == 0
        )
        fits = 2 * ranks * rows * share < 40 * 1024 * 1024
        if aligned and fits:
            return with_kernel(ranks, teams, weight_up, low_up, high_up, norm_train, norm_step)
        return with_collectives(weight_up, low_up, high_up, norm_train, norm_step)

    in_specs = (
        P("rows", "cols"),
        P("rows", None),
        P(None, "cols"),
        P(("rows", "cols")),
        P(("rows", "cols")),
    )
    out_specs = (P(None, ("cols", "rows")), P(("cols", "rows")), P())
    return jax.shard_map(
        per_device, mesh=mesh, in_specs=in_specs, out_specs=out_specs, check_vma=False
    )
```

time: 838 us -> 829 us (0.989)
    pallas_call x2 -> x4, Pallas kernels: 836 us -> 829 us  [the longest x2 815 us: call(): pl.pallas_call(functools.partial(exchange, ranks, teams, first), out_shap...]
where the time goes in v1:
time: 829 us
  Pallas kernels  829 us (100%)
    pallas_call x2, Pallas kernels, call(): pl.pallas_call(functools.partial(exchange, ranks, teams, first), out_shap...  815 us

profile of v1, /device:TPU:0, one launch (start us, length us, event | category | flops | bytes accessed | tf_op | source)
XLA Modules:
  0.0 829.3 jit_solution(5188643091654329182)
XLA Ops:
  0.6 706.0 %shard_map.76 = (bf16[11,12288,128]{2,1,0:T(8,128)(2,1)S(1)}, f32[12,128]{1,0:T(8,128)}, bf16[4,8,64,384]{3,2,1,0:T(8,128)(2,1)}, bf16[96,128]{1,0:T(8,128)(2,1)}) custom-call(bf16[1536,12288]{1,0:T(8,128)(2,1)} %refs_0_.3, bf16[64,1536]{1,0:T(8,128)(2,1)} %bitcast.5, bf16[64,12288]{1,0:T(8,128)(2,1)} %refs_2_.3, f32[3,128]{1,0:T(4,128)} %bitcast.6, ...), custom_call_target="tpu_custom_call" | custom-call | tf_op jit(solution)/shard_map/pallas_call | solution.py:329
  706.7 10.5 %shard_map.77 = (bf16[12288,1536]{1,0:T(8,128)(2,1)}, f32[12,128]{1,0:T(8,128)}, bf16[96,128]{1,0:T(8,128)(2,1)}) custom-call(bf16[11,12288,128]{2,1,0:T(8,128)(2,1)S(1)} %get-tuple-element.14.held, f32[12,128]{1,0:T(8,128)} %get-tuple-element.15.scale_ref, bf16[96,128]{1,0:T(8,128)(2,1)} %get-tuple-element.16.norm_ref), custom_call_target="tpu_custom_call" | custom-call | tf_op jit(solution)/shard_map/pallas_call | solution.py:361
  717.1 109.4 %shard_map.78 = (bf16[2,12288,128]{2,1,0:T(8,128)(2,1)S(1)}, f32[12,128]{1,0:T(8,128)}) custom-call(bf16[1536,12288]{1,0:T(8,128)(2,1)} %refs_0_.3, bf16[4,8,64,384]{3,2,1,0:T(8,128)(2,1)} %get-tuple-element.18.refs_1_, bf16[64,12288]{1,0:T(8,128)(2,1)} %refs_2_.3, f32[12,128]{1,0:T(8,128)} %get-tuple-element.19.refs_3_), custom_call_target="tpu_custom_call" | custom-call | tf_op jit(solution)/shard_map/pallas_call | solution.py:329
  826.5 2.7 shard_map.79

commit v2 on v1

--- a/solution.py
+++ b/solution.py
@@ -29,7 +29,7 @@
 
 
 def cut(pieces):
-    return pieces - 2 + lax.rem(lax.axis_index("cols"), 2)
+    return pieces - 1 - lax.rem(lax.axis_index("cols"), 2)
 
 
 def exchange(ranks, teams, first, *refs):
@@ -154,11 +154,10 @@
         direct = [half] + list(range(1, half))
         for step in direct:
             low_copy(low_mine, me, partner(me, step), step).start()
+        issue(low)
         for step in range(1, ranks):
             for which in range(2):
                 norm_copy(which, partner(me, step), me).start()
-
-        issue(low)
 
         low_copy(low_mine, across, across, half).wait_recv()
         for step in range(1, half):
@@ -220,23 +219,35 @@
 
     puts = start_first() if first else start_second()
 
+    def span(owner, quarter):
+        return pl.ds(pl.multiple_of(owner * rows + quarter * part, 16), part)
+
+    def prepare(piece):
+        now_high = high_own[:, pl.ds(pl.multiple_of(piece * LANES, LANES), LANES)]
+
+        @pl.loop(0, ranks)
+        def _(owner):
+            @pl.loop(0, teams)
+            def _(quarter):
+                fresh[span(owner, quarter), :] = mix_rate * lax.dot_general(
+                    low_all[quarter, owner], now_high, (((0,), (0,)), ((), ())),
+                    preferred_element_type=jnp.float32,
+                )
+
     def gather_block(piece, owner, total):
-        now_high = high_own[:, pl.ds(pl.multiple_of(piece * LANES, LANES), LANES)]
-
         def one(quarter, total):
-            added = lax.dot_general(
-                low_all[quarter, owner], now_high, (((0,), (0,)), ((), ())),
-                preferred_element_type=jnp.float32,
-            )
-            span = pl.ds(pl.multiple_of(owner * rows + quarter * part, 16), part)
-            now = held[piece - low, span, :].astype(jnp.float32) + mix_rate * added
-            fresh[span, :] = now
+            at = span(owner, quarter)
+            now = held[piece - low, at, :].astype(jnp.float32) + fresh[at, :]
+            fresh[at, :] = now
             return total + jnp.sum((now * now).reshape(part // 8, 8, LANES), axis=0)
 
         return lax.fori_loop(0, teams, one, total)
+
+    scale_put = pltpu.make_async_copy(scale_ref, scale_out, small_sem.at[0])
 
     @pl.loop(low, high)
     def _(piece):
+        prepare(piece)
         piece_own(piece).wait()
         total = gather_block(piece, me, jnp.zeros((8, LANES), jnp.float32))
         for back in arrivals:
@@ -246,13 +257,16 @@
         scale_ref[pl.ds(piece, 1), :] = scale
         inverse = 1.0 / scale
 
-        @pl.loop(0, ranks * teams)
-        def _(index):
-            span = pl.ds(pl.multiple_of(index * part, 16), part)
-            held[piece - low, span, :] = (fresh[span, :] * inverse).astype(jnp.bfloat16)
-
-    scale_put = pltpu.make_async_copy(scale_ref, scale_out, small_sem.at[0])
-    scale_put.start()
+        @pl.loop(0, ranks)
+        def _(owner):
+            @pl.loop(0, teams)
+            def _(quarter):
+                at = span(owner, quarter)
+                held[piece - low, at, :] = (fresh[at, :] * inverse).astype(jnp.bfloat16)
+
+            @pl.when(jnp.logical_and(piece == high - 1, owner == 0))
+            def _():
+                scale_put.start()
 
     @pl.loop(low, high)
     def _(piece):

time: 829 us -> 826 us (level)
  Pallas kernels: 829 us -> 818 us
    pallas_call x2, Pallas kernels: 815 us -> 805 us  [call(): pl.pallas_call(functools.partial(exchange, ranks, teams, first), out_shap...]
where the time goes in v2:
time: 826 us; the launch traced here: 819 us
  Pallas kernels  818 us (99%)
    pallas_call x2, Pallas kernels, call(): pl.pallas_call(functools.partial(exchange, ranks, teams, first), out_shap...  805 us

profile of v2, /device:TPU:0, one launch (start us, length us, event | category | flops | bytes accessed | tf_op | source)
XLA Modules:
  0.0 818.6 jit_solution(15189943273589271231)
XLA Ops:
  0.6 721.6 %shard_map.76 = (bf16[11,12288,128]{2,1,0:T(8,128)(2,1)S(1)}, f32[12,128]{1,0:T(8,128)}, bf16[4,8,64,384]{3,2,1,0:T(8,128)(2,1)}, bf16[96,128]{1,0:T(8,128)(2,1)}) custom-call(bf16[1536,12288]{1,0:T(8,128)(2,1)} %refs_0_.3, bf16[64,1536]{1,0:T(8,128)(2,1)} %bitcast.5, bf16[64,12288]{1,0:T(8,128)(2,1)} %refs_2_.3, f32[3,128]{1,0:T(4,128)} %bitcast.6, ...), custom_call_target="tpu_custom_call" | custom-call | tf_op jit(solution)/shard_map/pallas_call | solution.py:343
  722.2 11.4 %shard_map.77 = (bf16[12288,1536]{1,0:T(8,128)(2,1)}, f32[12,128]{1,0:T(8,128)}, bf16[96,128]{1,0:T(8,128)(2,1)}) custom-call(bf16[11,12288,128]{2,1,0:T(8,128)(2,1)S(1)} %get-tuple-element.14.held, f32[12,128]{1,0:T(8,128)} %get-tuple-element.15.scale_ref, bf16[96,128]{1,0:T(8,128)(2,1)} %get-tuple-element.16.norm_ref), custom_call_target="tpu_custom_call" | custom-call | tf_op jit(solution)/shard_map/pallas_call | solution.py:375
  733.6 83.2 %shard_map.78 = (bf16[2,12288,128]{2,1,0:T(8,128)(2,1)S(1)}, f32[12,128]{1,0:T(8,128)}) custom-call(bf16[1536,12288]{1,0:T(8,128)(2,1)} %refs_0_.3, bf16[4,8,64,384]{3,2,1,0:T(8,128)(2,1)} %get-tuple-element.18.refs_1_, bf16[64,12288]{1,0:T(8,128)(2,1)} %refs_2_.3, f32[12,128]{1,0:T(8,128)} %get-tuple-element.19.refs_3_), custom_call_target="tpu_custom_call" | custom-call | tf_op jit(solution)/shard_map/pallas_call | solution.py:343
  816.9 1.7 shard_map.79

commit v3 on v2

--- a/solution.py
+++ b/solution.py
@@ -16,16 +16,17 @@
     bit, other = 1, me
     while bit <= step:
         if step & bit:
-            other = other + bit - 2 * bit * lax.rem(other // bit, 2)
+            other = other + bit - 2 * bit * lax.rem(me // bit, 2)
         bit *= 2
     return other
 
 
-def send_orders(ranks):
+def send_orders(ranks, first):
     far, near = list(range(ranks - 1, ranks // 2 - 1, -1)), list(range(ranks // 2 - 1, 0, -1))
     half = len(far) // 2
     turned = near[:-1][::-1] + near[-1:]
-    return far + near, far[half:] + far[:half] + turned
+    other = far[half:] + far[:half] + turned
+    return (far + near if first else near + far), other
 
 
 def cut(pieces):
@@ -62,8 +63,14 @@
         one, other = partner(me, one), partner(me, other)
         return one + parity * (other - one)
 
-    peers = [pick(one, other) for one, other in zip(*send_orders(ranks))]
-    arrivals = peers[half:][::-1] + peers[:half]
+    orders = send_orders(ranks, first)
+    peers = [pick(one, other) for one, other in zip(*orders)]
+    arrivals = [
+        pick(one, other)
+        for one, other in zip(
+            *[sorted(order, key=lambda step: step >= half) for order in orders]
+        )
+    ]
 
     def window(owner, piece):
         return pl.ds(pl.multiple_of(owner * share + piece * LANES, LANES), LANES)
@@ -122,15 +129,27 @@
                 device_id_type=MESH,
             )
 
-        def norm_copy(which, to, source_rank):
+        def norm_copy(which, source, owner, to, sem):
             return pltpu.make_async_remote_copy(
-                src_ref=gains[which],
-                dst_ref=norm_all.at[which, team, me],
-                send_sem=norm_send.at[which, to],
-                recv_sem=norm_recv.at[which, source_rank],
+                src_ref=source,
+                dst_ref=norm_all.at[which, team, owner],
+                send_sem=norm_send.at[which, sem],
+                recv_sem=norm_recv.at[which, owner],
                 device_id={"rows": to},
                 device_id_type=MESH,
             )
+
+        def own(to, sem, owner):
+            return [low_copy(low_mine, owner, to, sem)] + [
+                norm_copy(which, gains[which], owner, to, sem) for which in range(2)
+            ]
+
+        def passed_on(step):
+            to, sem = partner(me, step), half + step
+            return [low_copy(low_all.at[team, across], across, to, sem)] + [
+                norm_copy(which, norm_all.at[which, team, across], across, to, sem)
+                for which in range(2)
+            ]
 
         def team_copy(buffer, sends, receives, to, source_team):
             return pltpu.make_async_remote_copy(
@@ -153,29 +172,30 @@
         across = partner(me, half)
         direct = [half] + list(range(1, half))
         for step in direct:
-            low_copy(low_mine, me, partner(me, step), step).start()
+            for copy in own(partner(me, step), step, me):
+                copy.start()
+
         issue(low)
-        for step in range(1, ranks):
-            for which in range(2):
-                norm_copy(which, partner(me, step), me).start()
-
-        low_copy(low_mine, across, across, half).wait_recv()
+
+        for copy in own(across, half, across):
+            copy.wait_recv()
         for step in range(1, half):
-            low_copy(low_all.at[team, across], across, partner(me, step), half + step).start()
+            for copy in passed_on(step):
+                copy.start()
 
         pl.loop(low + 1, high)(issue)
 
         for copy in keeps:
             copy.wait()
         for step in direct:
-            low_copy(low_mine, me, partner(me, step), step).wait_send()
+            for copy in own(partner(me, step), step, me):
+                copy.wait_send()
         for step in range(1, half):
-            low_copy(low_mine, partner(me, step), across, step).wait_recv()
-            low_copy(low_mine, partner(me, half + step), across, step).wait_recv()
-            low_copy(low_all.at[team, across], across, partner(me, step), half + step).wait_send()
-        for step in range(1, ranks):
-            for which in range(2):
-                norm_copy(which, partner(me, step), partner(me, step)).wait()
+            for owner in (partner(me, step), partner(me, half + step)):
+                for copy in own(across, step, owner):
+                    copy.wait_recv()
+            for copy in passed_on(step):
+                copy.wait_send()
         high_copy.wait()
 
         gathers = [(low_all, low_send2, low_recv2)] + [

time: 826 us -> 821 us (level)
  no operation moved by 1% of the time
where the time goes in v3:
time: 821 us; the launch traced here: 815 us
  Pallas kernels  814 us (99%)
    pallas_call x2, Pallas kernels, call(): pl.pallas_call(functools.partial(exchange, ranks, teams, first), out_shap...  801 us

profile of v3, /device:TPU:0, one launch (start us, length us, event | category | flops | bytes accessed | tf_op | source)
XLA Modules:
  0.0 814.8 jit_solution(1962124005316911202)
XLA Ops:
  0.6 721.3 %shard_map.76 = (bf16[11,12288,128]{2,1,0:T(8,128)(2,1)S(1)}, f32[12,128]{1,0:T(8,128)}, bf16[4,8,64,384]{3,2,1,0:T(8,128)(2,1)}, bf16[96,128]{1,0:T(8,128)(2,1)}) custom-call(bf16[1536,12288]{1,0:T(8,128)(2,1)} %refs_0_.3, bf16[64,1536]{1,0:T(8,128)(2,1)} %bitcast.5, bf16[64,12288]{1,0:T(8,128)(2,1)} %refs_2_.3, f32[3,128]{1,0:T(4,128)} %bitcast.6, ...), custom_call_target="tpu_custom_call" | custom-call | tf_op jit(solution)/shard_map/pallas_call | solution.py:363
  721.9 11.4 %shard_map.77 = (bf16[12288,1536]{1,0:T(8,128)(2,1)}, f32[12,128]{1,0:T(8,128)}, bf16[96,128]{1,0:T(8,128)(2,1)}) custom-call(bf16[11,12288,128]{2,1,0:T(8,128)(2,1)S(1)} %get-tuple-element.14.held, f32[12,128]{1,0:T(8,128)} %get-tuple-element.15.scale_ref, bf16[96,128]{1,0:T(8,128)(2,1)} %get-tuple-element.16.norm_ref), custom_call_target="tpu_custom_call" | custom-call | tf_op jit(solution)/shard_map/pallas_call | solution.py:395
  733.3 79.7 %shard_map.78 = (bf16[2,12288,128]{2,1,0:T(8,128)(2,1)S(1)}, f32[12,128]{1,0:T(8,128)}) custom-call(bf16[1536,12288]{1,0:T(8,128)(2,1)} %refs_0_.3, bf16[4,8,64,384]{3,2,1,0:T(8,128)(2,1)} %get-tuple-element.18.refs_1_, bf16[64,12288]{1,0:T(8,128)(2,1)} %refs_2_.3, f32[12,128]{1,0:T(8,128)} %get-tuple-element.19.refs_3_), custom_call_target="tpu_custom_call" | custom-call | tf_op jit(solution)/shard_map/pallas_call | solution.py:363
  813.1 1.7 shard_map.79
